TPU v7x, 32 devices: a whole 2x2x4 slice. The times are simulated.
32 devices in a mesh: gx: 8 (over z, y), gy: 4 (over x, core).
Axes of the slice: x: 2, y: 2, z: 4, core: 2. Of those that a mesh axis runs over, the one named last changes fastest.
Arguments:
- anomalies: float32 [80, 16, 32, 128], P(None, 'gx', 'gy'), may hold values from -6 to 6
- state_mean: float32 [16, 32, 128], P('gx', 'gy'), may hold values from -6 to 6
- obs_value: float32 [16, 256], P(None, 'gy'), may hold values from -8 to 8
- obs_cell: int32 [16, 256], replicated, may hold values from 0 to 2047
- owner: int32 [16], replicated, may hold values from 0 to 7, as said below
- order: int32 [16], replicated, may hold values from 0 to 15, each once
- root_inv: float32 [16, 256, 256], P(None, 'gy'), as said below
- gain_inv: float32 [16, 256, 256], P(None, 'gy'), as said below
Outputs:
- post_anomalies: float32 [80, 16, 32, 128], P(None, 'gx', 'gy')
- post_mean: float32 [16, 32, 128], P('gx', 'gy')
Inputs may be any that keep to these rules, and one draw needn't show every extreme that they name: `owner`: some batch lies at slab 8 - 2, some at slab 1 and some at slab 8 // 2; the others favour low slabs. `order`: each batch number once. `root_inv`: symmetric. `gain_inv`: symmetric.
All inputs are finite; a program needn't handle non-finite values.
Results may differ from a plain program's by a relative error of at most 0.0001.
Values sent between devices are 32-bit elements; how exact they have to be, the bound alone decides.
A program may use at most 64 MiB of HBM per device.

v0:
```python
import jax
import jax.numpy as jnp
from jax import lax
from jax.sharding import PartitionSpec as P

BATCHES = 16
REACH = 3


def shifted(value, axis, steps):
    count = lax.axis_size(axis)
    pairs = [(source, (source + steps) % count) for source in range(count)]
    return lax.ppermute(value, axis, pairs)


def product(left_side, right_side):
    return jnp.dot(
        left_side, right_side, precision=lax.Precision.HIGHEST, preferred_element_type=jnp.float32
    )


def prior_direct(masked):
    total = masked
    for step in range(1, REACH + 1):
        for sign_step in [step, -step]:
            total = total + shifted(masked, "gx", sign_step)
    return total


def local(anomalies, state_mean, obs_value, obs_cell, owner, order, root_inv, gain_inv):
    members, lon_dev, lat_dev, levels = anomalies.shape
    cell_count = lon_dev * lat_dev * levels
    quarter = obs_value.shape[1]
    obs_total = obs_cell.shape[1]
    slab_count = lax.axis_size("gx")
    band_count = lax.axis_size("gy")
    column = lax.axis_index("gx")
    band_index = lax.axis_index("gy")
    lon_total = slab_count * lon_dev
    lat_total = band_count * lat_dev
    taper_span = REACH * lon_dev + 1.0
    cell_ids = jnp.arange(cell_count, dtype=jnp.int32)
    cell_lon = column * lon_dev + cell_ids // (lat_dev * levels)
    cell_lat = band_index * lat_dev + cell_ids // levels % lat_dev
    obs_band = jnp.arange(obs_total, dtype=jnp.int32) // quarter

    def assimilate(batch_turn, carried):
        state_rows, mean_row = carried
        batch_id = order[batch_turn]
        root_slab = owner[batch_id]
        is_root = column == root_slab
        cells_of = obs_cell[batch_id]
        local_ids = lax.dynamic_slice_in_dim(cells_of, band_index * quarter, quarter)
        picked = jnp.take(state_rows, local_ids, axis=1)
        innovation = obs_value[batch_id] - jnp.take(mean_row, local_ids)
        root_rows = root_inv[batch_id]
        gain_rows = gain_inv[batch_id]
        joined = jnp.concatenate([picked, innovation[None, :]], axis=0)
        masked = jnp.where(is_root, joined, jnp.zeros_like(joined))
        joined = prior_direct(masked)
        picked, innovation = (joined[:members], joined[members])
        prior_all, innov_all = (
            lax.all_gather(picked, "gy", axis=1, tiled=True),
            lax.all_gather(innovation, "gy", axis=0, tiled=True),
        )
        weighted = product(prior_all, root_rows.T)
        gain_part = product(gain_rows, innov_all)
        weighted_all, gain_all = (
            lax.all_gather(weighted, "gy", axis=1, tiled=True),
            lax.all_gather(gain_part, "gy", axis=0, tiled=True),
        )
        obs_lon = root_slab * lon_dev + cells_of // (lat_dev * levels)
        obs_lat = obs_band * lat_dev + cells_of // levels % lat_dev
        slab_gap = jnp.abs(column - root_slab)
        in_reach = jnp.minimum(slab_gap, slab_count - slab_gap) <= REACH

        def near_update(operands):
            rows_now, mean_now = operands
            lon_gap = jnp.abs(obs_lon[:, None] - cell_lon[None, :])
            cycle_gap = jnp.minimum(lon_gap, lon_total - lon_gap)
            lat_gap = jnp.abs(obs_lat[:, None] - cell_lat[None, :])
            taper_rows = jnp.maximum(0.0, 1.0 - cycle_gap.astype(jnp.float32) / taper_span) * (
                1.0 - lat_gap.astype(jnp.float32) / lat_total
            )
            covariance = product(prior_all.T, rows_now) / (members - 1.0)
            gained = taper_rows * covariance
            stacked = jnp.concatenate([weighted_all, gain_all[None, :]], axis=0)
            increment = product(stacked, gained)
            return (rows_now - increment[:members], mean_now + increment[members])

        def keep_all(operands):
            return operands

        return lax.cond(in_reach, near_update, keep_all, (state_rows, mean_row))

    start_rows = anomalies.reshape(members, cell_count)
    start_mean = state_mean.reshape(cell_count)
    final_rows, final_mean = lax.fori_loop(0, BATCHES, assimilate, (start_rows, start_mean))
    return (
        final_rows.reshape(members, lon_dev, lat_dev, levels),
        final_mean.reshape(lon_dev, lat_dev, levels),
    )


def solution(mesh):
    return jax.shard_map(
        local,
        mesh=mesh,
        in_specs=(
            P(None, "gx", "gy", None),
            P("gx", "gy", None),
            P(None, "gy"),
            P(),
            P(),
            P(),
            P(None, "gy", None),
            P(None, "gy", None),
        ),
        out_specs=(P(None, "gx", "gy", None), P("gx", "gy", None)),
        check_vma=False,
    )
```

profile of v0, /device:TPU:0, one launch (start us, length us, event | category | flops | bytes accessed | tf_op | source)
XLA Modules:
  0.0 853.1 jit_solution(17424836850244703015)
XLA Ops:
  3.4 848.7 %while.19 = (s32[]{:T(128)}, f32[80,2048]{1,0:T(8,128)S(1)}, f32[2048]{0:T(1024)S(1)}, s32[16]{0:T(128)}, s32[16]{0:T(128)}, /*index=5*/s32[]{:T(128)}, s32[16,2...) while((s32[]{:T(128)}, f32[80,2048]{1,0:T(8,128)S(1)}, ...), condition=%wide.region_3.4_spmd.clone, body=%wide.region_0.3_spmd.clone.sunk | while | flops 1037555904 | bytes 10573724 | solution.py:98
  27.9 5.6 all-reduce.6
  34.7 6.7 all-reduce.7
  41.4 5.4 all_gather.48
  47.9 5.4 all_gather.49
  81.8 5.6 all-reduce.6
  88.7 6.1 all-reduce.7
  94.8 5.4 all_gather.48
  101.2 5.4 all_gather.49
  135.2 5.6 all-reduce.6
  142.0 6.6 all-reduce.7
  148.6 5.4 all_gather.48
  155.0 5.4 all_gather.49
  189.0 5.6 all-reduce.6
  195.8 6.1 all-reduce.7
  201.9 5.4 all_gather.48
  208.4 5.4 all_gather.49
  242.3 5.6 all-reduce.6
  249.2 6.6 all-reduce.7
  255.7 5.4 all_gather.48
  262.2 5.4 all_gather.49
  296.1 5.6 all-reduce.6
  303.0 6.1 all-reduce.7
  309.1 5.4 all_gather.48
  315.6 5.4 all_gather.49
  349.5 5.6 all-reduce.6
  356.3 6.6 all-reduce.7
  362.9 5.4 all_gather.48
  369.4 5.4 all_gather.49
  400.3 5.6 all-reduce.6
  407.2 6.1 all-reduce.7
  413.3 5.4 all_gather.48
  419.8 5.4 all_gather.49
  433.3 7.4 collective-permute-start.5
  452.5 5.6 all-reduce.6
  459.3 6.6 all-reduce.7
  465.9 5.4 all_gather.48
  472.4 5.4 all_gather.49
  506.3 5.6 all-reduce.6
  513.1 6.1 all-reduce.7
  519.3 5.4 all_gather.48
  525.7 5.4 all_gather.49
  559.6 5.6 all-reduce.6
  566.5 6.6 all-reduce.7
  573.1 5.4 all_gather.48
  579.5 5.4 all_gather.49
  613.5 5.6 all-reduce.6
  620.3 6.1 all-reduce.7
  626.4 5.4 all_gather.48
  632.9 5.4 all_gather.49
  663.9 5.6 all-reduce.6
  670.7 6.6 all-reduce.7
  683.8 5.4 all_gather.49
  717.7 5.6 all-reduce.6
  724.5 6.1 all-reduce.7
  737.1 5.4 all_gather.49
  771.0 5.6 all-reduce.6
  777.9 6.6 all-reduce.7
  784.5 5.4 all_gather.48
  790.9 5.4 all_gather.49
  821.9 5.6 all-reduce.6
  828.8 6.1 all-reduce.7
  834.9 5.4 all_gather.48
  841.3 5.4 all_gather.49
  (871 shorter events, 486.8 us)
Async XLA Ops:
  11.5 9.9 %collective-permute-start.5 = (f32[81,64]{0,1:T(8,128)S(1)}, f32[81,64]{0,1:T(8,128)S(1)}, u32[]{:S(2)}, u32[]{:S(2)}) collective-permute-start(f32[81,64]{0,1:T(8,128)S(1)} %maximum_select_fusion.2), channel_id=1, source_target_pairs={{0,4},{4,8},{8,12},{12,16},{16,20},{20,24},{24,28},{28,0},{1,5},{5... | collective-permute-start | bytes 62216 | tf_op jit(solution)/shard_map/while/body/eval_jaxpr/ppermute | solution.py:13
  14.5 12.8 %collective-permute-start.4 = (f32[81,64]{0,1:T(8,128)S(1)}, f32[81,64]{0,1:T(8,128)S(1)}, u32[]{:S(2)}, u32[]{:S(2)}) collective-permute-start(f32[81,64]{0,1:T(8,128)S(1)} %maximum_select_fusion.2), channel_id=1, source_target_pairs={{0,28},{4,0},{8,4},{12,8},{16,12},{20,16},{24,20},{28,24},{1,29},{... | collective-permute-start | bytes 62216 | tf_op jit(solution)/shard_map/while/body/eval_jaxpr/ppermute | solution.py:13
  17.6 9.7 %collective-permute-start.3 = (f32[81,64]{0,1:T(8,128)S(1)}, f32[81,64]{0,1:T(8,128)S(1)}, u32[]{:S(2)}, u32[]{:S(2)}) collective-permute-start(f32[81,64]{0,1:T(8,128)S(1)} %maximum_select_fusion.2), channel_id=1, source_target_pairs={{0,8},{4,12},{8,16},{12,20},{16,24},{20,28},{24,0},{28,4},{1,9},{5... | collective-permute-start | bytes 62216 | tf_op jit(solution)/shard_map/while/body/eval_jaxpr/ppermute | solution.py:13
  17.6 9.7 %collective-permute-start.2 = (f32[81,64]{0,1:T(8,128)S(1)}, f32[81,64]{0,1:T(8,128)S(1)}, u32[]{:S(2)}, u32[]{:S(2)}) collective-permute-start(f32[81,64]{0,1:T(8,128)S(1)} %maximum_select_fusion.2), channel_id=1, source_target_pairs={{0,24},{4,28},{8,0},{12,4},{16,8},{20,12},{24,16},{28,20},{1,25},{... | collective-permute-start | bytes 62216 | tf_op jit(solution)/shard_map/while/body/eval_jaxpr/ppermute | solution.py:13
  66.8 8.6 %collective-permute-start.5 = (f32[81,64]{0,1:T(8,128)S(1)}, f32[81,64]{0,1:T(8,128)S(1)}, u32[]{:S(2)}, u32[]{:S(2)}) collective-permute-start(f32[81,64]{0,1:T(8,128)S(1)} %maximum_select_fusion.2), channel_id=1, source_target_pairs={{0,4},{4,8},{8,12},{12,16},{16,20},{20,24},{24,28},{28,0},{1,5},{5... | collective-permute-start | bytes 62216 | tf_op jit(solution)/shard_map/while/body/eval_jaxpr/ppermute | solution.py:13
  67.2 14.1 %collective-permute-start.4 = (f32[81,64]{0,1:T(8,128)S(1)}, f32[81,64]{0,1:T(8,128)S(1)}, u32[]{:S(2)}, u32[]{:S(2)}) collective-permute-start(f32[81,64]{0,1:T(8,128)S(1)} %maximum_select_fusion.2), channel_id=1, source_target_pairs={{0,28},{4,0},{8,4},{12,8},{16,12},{20,16},{24,20},{28,24},{1,29},{... | collective-permute-start | bytes 62216 | tf_op jit(solution)/shard_map/while/body/eval_jaxpr/ppermute | solution.py:13
  71.5 9.7 %collective-permute-start.3 = (f32[81,64]{0,1:T(8,128)S(1)}, f32[81,64]{0,1:T(8,128)S(1)}, u32[]{:S(2)}, u32[]{:S(2)}) collective-permute-start(f32[81,64]{0,1:T(8,128)S(1)} %maximum_select_fusion.2), channel_id=1, source_target_pairs={{0,8},{4,12},{8,16},{12,20},{16,24},{20,28},{24,0},{28,4},{1,9},{5... | collective-permute-start | bytes 62216 | tf_op jit(solution)/shard_map/while/body/eval_jaxpr/ppermute | solution.py:13
  71.5 9.7 %collective-permute-start.2 = (f32[81,64]{0,1:T(8,128)S(1)}, f32[81,64]{0,1:T(8,128)S(1)}, u32[]{:S(2)}, u32[]{:S(2)}) collective-permute-start(f32[81,64]{0,1:T(8,128)S(1)} %maximum_select_fusion.2), channel_id=1, source_target_pairs={{0,24},{4,28},{8,0},{12,4},{16,8},{20,12},{24,16},{28,20},{1,25},{... | collective-permute-start | bytes 62216 | tf_op jit(solution)/shard_map/while/body/eval_jaxpr/ppermute | solution.py:13
  120.2 8.6 %collective-permute-start.5 = (f32[81,64]{0,1:T(8,128)S(1)}, f32[81,64]{0,1:T(8,128)S(1)}, u32[]{:S(2)}, u32[]{:S(2)}) collective-permute-start(f32[81,64]{0,1:T(8,128)S(1)} %maximum_select_fusion.2), channel_id=1, source_target_pairs={{0,4},{4,8},{8,12},{12,16},{16,20},{20,24},{24,28},{28,0},{1,5},{5... | collective-permute-start | bytes 62216 | tf_op jit(solution)/shard_map/while/body/eval_jaxpr/ppermute | solution.py:13
  120.2 14.4 %collective-permute-start.4 = (f32[81,64]{0,1:T(8,128)S(1)}, f32[81,64]{0,1:T(8,128)S(1)}, u32[]{:S(2)}, u32[]{:S(2)}) collective-permute-start(f32[81,64]{0,1:T(8,128)S(1)} %maximum_select_fusion.2), channel_id=1, source_target_pairs={{0,28},{4,0},{8,4},{12,8},{16,12},{20,16},{24,20},{28,24},{1,29},{... | collective-permute-start | bytes 62216 | tf_op jit(solution)/shard_map/while/body/eval_jaxpr/ppermute | solution.py:13
  124.9 9.7 %collective-permute-start.3 = (f32[81,64]{0,1:T(8,128)S(1)}, f32[81,64]{0,1:T(8,128)S(1)}, u32[]{:S(2)}, u32[]{:S(2)}) collective-permute-start(f32[81,64]{0,1:T(8,128)S(1)} %maximum_select_fusion.2), channel_id=1, source_target_pairs={{0,8},{4,12},{8,16},{12,20},{16,24},{20,28},{24,0},{28,4},{1,9},{5... | collective-permute-start | bytes 62216 | tf_op jit(solution)/shard_map/while/body/eval_jaxpr/ppermute | solution.py:13
  124.9 9.7 %collective-permute-start.2 = (f32[81,64]{0,1:T(8,128)S(1)}, f32[81,64]{0,1:T(8,128)S(1)}, u32[]{:S(2)}, u32[]{:S(2)}) collective-permute-start(f32[81,64]{0,1:T(8,128)S(1)} %maximum_select_fusion.2), channel_id=1, source_target_pairs={{0,24},{4,28},{8,0},{12,4},{16,8},{20,12},{24,16},{28,20},{1,25},{... | collective-permute-start | bytes 62216 | tf_op jit(solution)/shard_map/while/body/eval_jaxpr/ppermute | solution.py:13
  174.0 8.6 %collective-permute-start.5 = (f32[81,64]{0,1:T(8,128)S(1)}, f32[81,64]{0,1:T(8,128)S(1)}, u32[]{:S(2)}, u32[]{:S(2)}) collective-permute-start(f32[81,64]{0,1:T(8,128)S(1)} %maximum_select_fusion.2), channel_id=1, source_target_pairs={{0,4},{4,8},{8,12},{12,16},{16,20},{20,24},{24,28},{28,0},{1,5},{5... | collective-permute-start | bytes 62216 | tf_op jit(solution)/shard_map/while/body/eval_jaxpr/ppermute | solution.py:13
  174.0 14.4 %collective-permute-start.4 = (f32[81,64]{0,1:T(8,128)S(1)}, f32[81,64]{0,1:T(8,128)S(1)}, u32[]{:S(2)}, u32[]{:S(2)}) collective-permute-start(f32[81,64]{0,1:T(8,128)S(1)} %maximum_select_fusion.2), channel_id=1, source_target_pairs={{0,28},{4,0},{8,4},{12,8},{16,12},{20,16},{24,20},{28,24},{1,29},{... | collective-permute-start | bytes 62216 | tf_op jit(solution)/shard_map/while/body/eval_jaxpr/ppermute | solution.py:13
  178.7 9.7 %collective-permute-start.3 = (f32[81,64]{0,1:T(8,128)S(1)}, f32[81,64]{0,1:T(8,128)S(1)}, u32[]{:S(2)}, u32[]{:S(2)}) collective-permute-start(f32[81,64]{0,1:T(8,128)S(1)} %maximum_select_fusion.2), channel_id=1, source_target_pairs={{0,8},{4,12},{8,16},{12,20},{16,24},{20,28},{24,0},{28,4},{1,9},{5... | collective-permute-start | bytes 62216 | tf_op jit(solution)/shard_map/while/body/eval_jaxpr/ppermute | solution.py:13
  178.7 9.7 %collective-permute-start.2 = (f32[81,64]{0,1:T(8,128)S(1)}, f32[81,64]{0,1:T(8,128)S(1)}, u32[]{:S(2)}, u32[]{:S(2)}) collective-permute-start(f32[81,64]{0,1:T(8,128)S(1)} %maximum_select_fusion.2), channel_id=1, source_target_pairs={{0,24},{4,28},{8,0},{12,4},{16,8},{20,12},{24,16},{28,20},{1,25},{... | collective-permute-start | bytes 62216 | tf_op jit(solution)/shard_map/while/body/eval_jaxpr/ppermute | solution.py:13
  227.3 8.6 %collective-permute-start.5 = (f32[81,64]{0,1:T(8,128)S(1)}, f32[81,64]{0,1:T(8,128)S(1)}, u32[]{:S(2)}, u32[]{:S(2)}) collective-permute-start(f32[81,64]{0,1:T(8,128)S(1)} %maximum_select_fusion.2), channel_id=1, source_target_pairs={{0,4},{4,8},{8,12},{12,16},{16,20},{20,24},{24,28},{28,0},{1,5},{5... | collective-permute-start | bytes 62216 | tf_op jit(solution)/shard_map/while/body/eval_jaxpr/ppermute | solution.py:13
  227.3 14.4 %collective-permute-start.4 = (f32[81,64]{0,1:T(8,128)S(1)}, f32[81,64]{0,1:T(8,128)S(1)}, u32[]{:S(2)}, u32[]{:S(2)}) collective-permute-start(f32[81,64]{0,1:T(8,128)S(1)} %maximum_select_fusion.2), channel_id=1, source_target_pairs={{0,28},{4,0},{8,4},{12,8},{16,12},{20,16},{24,20},{28,24},{1,29},{... | collective-permute-start | bytes 62216 | tf_op jit(solution)/shard_map/while/body/eval_jaxpr/ppermute | solution.py:13
  232.1 9.7 %collective-permute-start.3 = (f32[81,64]{0,1:T(8,128)S(1)}, f32[81,64]{0,1:T(8,128)S(1)}, u32[]{:S(2)}, u32[]{:S(2)}) collective-permute-start(f32[81,64]{0,1:T(8,128)S(1)} %maximum_select_fusion.2), channel_id=1, source_target_pairs={{0,8},{4,12},{8,16},{12,20},{16,24},{20,28},{24,0},{28,4},{1,9},{5... | collective-permute-start | bytes 62216 | tf_op jit(solution)/shard_map/while/body/eval_jaxpr/ppermute | solution.py:13
  232.1 9.7 %collective-permute-start.2 = (f32[81,64]{0,1:T(8,128)S(1)}, f32[81,64]{0,1:T(8,128)S(1)}, u32[]{:S(2)}, u32[]{:S(2)}) collective-permute-start(f32[81,64]{0,1:T(8,128)S(1)} %maximum_select_fusion.2), channel_id=1, source_target_pairs={{0,24},{4,28},{8,0},{12,4},{16,8},{20,12},{24,16},{28,20},{1,25},{... | collective-permute-start | bytes 62216 | tf_op jit(solution)/shard_map/while/body/eval_jaxpr/ppermute | solution.py:13
  281.1 8.6 %collective-permute-start.5 = (f32[81,64]{0,1:T(8,128)S(1)}, f32[81,64]{0,1:T(8,128)S(1)}, u32[]{:S(2)}, u32[]{:S(2)}) collective-permute-start(f32[81,64]{0,1:T(8,128)S(1)} %maximum_select_fusion.2), channel_id=1, source_target_pairs={{0,4},{4,8},{8,12},{12,16},{16,20},{20,24},{24,28},{28,0},{1,5},{5... | collective-permute-start | bytes 62216 | tf_op jit(solution)/shard_map/while/body/eval_jaxpr/ppermute | solution.py:13
  281.1 14.4 %collective-permute-start.4 = (f32[81,64]{0,1:T(8,128)S(1)}, f32[81,64]{0,1:T(8,128)S(1)}, u32[]{:S(2)}, u32[]{:S(2)}) collective-permute-start(f32[81,64]{0,1:T(8,128)S(1)} %maximum_select_fusion.2), channel_id=1, source_target_pairs={{0,28},{4,0},{8,4},{12,8},{16,12},{20,16},{24,20},{28,24},{1,29},{... | collective-permute-start | bytes 62216 | tf_op jit(solution)/shard_map/while/body/eval_jaxpr/ppermute | solution.py:13
  285.9 9.7 %collective-permute-start.3 = (f32[81,64]{0,1:T(8,128)S(1)}, f32[81,64]{0,1:T(8,128)S(1)}, u32[]{:S(2)}, u32[]{:S(2)}) collective-permute-start(f32[81,64]{0,1:T(8,128)S(1)} %maximum_select_fusion.2), channel_id=1, source_target_pairs={{0,8},{4,12},{8,16},{12,20},{16,24},{20,28},{24,0},{28,4},{1,9},{5... | collective-permute-start | bytes 62216 | tf_op jit(solution)/shard_map/while/body/eval_jaxpr/ppermute | solution.py:13
  285.9 9.7 %collective-permute-start.2 = (f32[81,64]{0,1:T(8,128)S(1)}, f32[81,64]{0,1:T(8,128)S(1)}, u32[]{:S(2)}, u32[]{:S(2)}) collective-permute-start(f32[81,64]{0,1:T(8,128)S(1)} %maximum_select_fusion.2), channel_id=1, source_target_pairs={{0,24},{4,28},{8,0},{12,4},{16,8},{20,12},{24,16},{28,20},{1,25},{... | collective-permute-start | bytes 62216 | tf_op jit(solution)/shard_map/while/body/eval_jaxpr/ppermute | solution.py:13
  334.5 8.6 %collective-permute-start.5 = (f32[81,64]{0,1:T(8,128)S(1)}, f32[81,64]{0,1:T(8,128)S(1)}, u32[]{:S(2)}, u32[]{:S(2)}) collective-permute-start(f32[81,64]{0,1:T(8,128)S(1)} %maximum_select_fusion.2), channel_id=1, source_target_pairs={{0,4},{4,8},{8,12},{12,16},{16,20},{20,24},{24,28},{28,0},{1,5},{5... | collective-permute-start | bytes 62216 | tf_op jit(solution)/shard_map/while/body/eval_jaxpr/ppermute | solution.py:13
  334.5 14.4 %collective-permute-start.4 = (f32[81,64]{0,1:T(8,128)S(1)}, f32[81,64]{0,1:T(8,128)S(1)}, u32[]{:S(2)}, u32[]{:S(2)}) collective-permute-start(f32[81,64]{0,1:T(8,128)S(1)} %maximum_select_fusion.2), channel_id=1, source_target_pairs={{0,28},{4,0},{8,4},{12,8},{16,12},{20,16},{24,20},{28,24},{1,29},{... | collective-permute-start | bytes 62216 | tf_op jit(solution)/shard_map/while/body/eval_jaxpr/ppermute | solution.py:13
  339.2 9.7 %collective-permute-start.3 = (f32[81,64]{0,1:T(8,128)S(1)}, f32[81,64]{0,1:T(8,128)S(1)}, u32[]{:S(2)}, u32[]{:S(2)}) collective-permute-start(f32[81,64]{0,1:T(8,128)S(1)} %maximum_select_fusion.2), channel_id=1, source_target_pairs={{0,8},{4,12},{8,16},{12,20},{16,24},{20,28},{24,0},{28,4},{1,9},{5... | collective-permute-start | bytes 62216 | tf_op jit(solution)/shard_map/while/body/eval_jaxpr/ppermute | solution.py:13
  339.2 9.7 %collective-permute-start.2 = (f32[81,64]{0,1:T(8,128)S(1)}, f32[81,64]{0,1:T(8,128)S(1)}, u32[]{:S(2)}, u32[]{:S(2)}) collective-permute-start(f32[81,64]{0,1:T(8,128)S(1)} %maximum_select_fusion.2), channel_id=1, source_target_pairs={{0,24},{4,28},{8,0},{12,4},{16,8},{20,12},{24,16},{28,20},{1,25},{... | collective-permute-start | bytes 62216 | tf_op jit(solution)/shard_map/while/body/eval_jaxpr/ppermute | solution.py:13
  382.9 11.7 %collective-permute-start.5 = (f32[81,64]{0,1:T(8,128)S(1)}, f32[81,64]{0,1:T(8,128)S(1)}, u32[]{:S(2)}, u32[]{:S(2)}) collective-permute-start(f32[81,64]{0,1:T(8,128)S(1)} %maximum_select_fusion.2), channel_id=1, source_target_pairs={{0,4},{4,8},{8,12},{12,16},{16,20},{20,24},{24,28},{28,0},{1,5},{5... | collective-permute-start | bytes 62216 | tf_op jit(solution)/shard_map/while/body/eval_jaxpr/ppermute | solution.py:13
  386.6 12.7 %collective-permute-start.4 = (f32[81,64]{0,1:T(8,128)S(1)}, f32[81,64]{0,1:T(8,128)S(1)}, u32[]{:S(2)}, u32[]{:S(2)}) collective-permute-start(f32[81,64]{0,1:T(8,128)S(1)} %maximum_select_fusion.2), channel_id=1, source_target_pairs={{0,28},{4,0},{8,4},{12,8},{16,12},{20,16},{24,20},{28,24},{1,29},{... | collective-permute-start | bytes 62216 | tf_op jit(solution)/shard_map/while/body/eval_jaxpr/ppermute | solution.py:13
  389.7 9.7 %collective-permute-start.3 = (f32[81,64]{0,1:T(8,128)S(1)}, f32[81,64]{0,1:T(8,128)S(1)}, u32[]{:S(2)}, u32[]{:S(2)}) collective-permute-start(f32[81,64]{0,1:T(8,128)S(1)} %maximum_select_fusion.2), channel_id=1, source_target_pairs={{0,8},{4,12},{8,16},{12,20},{16,24},{20,28},{24,0},{28,4},{1,9},{5... | collective-permute-start | bytes 62216 | tf_op jit(solution)/shard_map/while/body/eval_jaxpr/ppermute | solution.py:13
  391.9 7.5 collective-permute-start.2
  433.3 12.7 %collective-permute-start.5 = (f32[81,64]{0,1:T(8,128)S(1)}, f32[81,64]{0,1:T(8,128)S(1)}, u32[]{:S(2)}, u32[]{:S(2)}) collective-permute-start(f32[81,64]{0,1:T(8,128)S(1)} %maximum_select_fusion.2), channel_id=1, source_target_pairs={{0,4},{4,8},{8,12},{12,16},{16,20},{20,24},{24,28},{28,0},{1,5},{5... | collective-permute-start | bytes 62216 | tf_op jit(solution)/shard_map/while/body/eval_jaxpr/ppermute | solution.py:13
  440.7 11.2 %collective-permute-start.4 = (f32[81,64]{0,1:T(8,128)S(1)}, f32[81,64]{0,1:T(8,128)S(1)}, u32[]{:S(2)}, u32[]{:S(2)}) collective-permute-start(f32[81,64]{0,1:T(8,128)S(1)} %maximum_select_fusion.2), channel_id=1, source_target_pairs={{0,28},{4,0},{8,4},{12,8},{16,12},{20,16},{24,20},{28,24},{1,29},{... | collective-permute-start | bytes 62216 | tf_op jit(solution)/shard_map/while/body/eval_jaxpr/ppermute | solution.py:13
  441.9 10.0 %collective-permute-start.3 = (f32[81,64]{0,1:T(8,128)S(1)}, f32[81,64]{0,1:T(8,128)S(1)}, u32[]{:S(2)}, u32[]{:S(2)}) collective-permute-start(f32[81,64]{0,1:T(8,128)S(1)} %maximum_select_fusion.2), channel_id=1, source_target_pairs={{0,8},{4,12},{8,16},{12,20},{16,24},{20,28},{24,0},{28,4},{1,9},{5... | collective-permute-start | bytes 62216 | tf_op jit(solution)/shard_map/while/body/eval_jaxpr/ppermute | solution.py:13
  443.3 8.6 %collective-permute-start.2 = (f32[81,64]{0,1:T(8,128)S(1)}, f32[81,64]{0,1:T(8,128)S(1)}, u32[]{:S(2)}, u32[]{:S(2)}) collective-permute-start(f32[81,64]{0,1:T(8,128)S(1)} %maximum_select_fusion.2), channel_id=1, source_target_pairs={{0,24},{4,28},{8,0},{12,4},{16,8},{20,12},{24,16},{28,20},{1,25},{... | collective-permute-start | bytes 62216 | tf_op jit(solution)/shard_map/while/body/eval_jaxpr/ppermute | solution.py:13
  491.3 8.6 %collective-permute-start.5 = (f32[81,64]{0,1:T(8,128)S(1)}, f32[81,64]{0,1:T(8,128)S(1)}, u32[]{:S(2)}, u32[]{:S(2)}) collective-permute-start(f32[81,64]{0,1:T(8,128)S(1)} %maximum_select_fusion.2), channel_id=1, source_target_pairs={{0,4},{4,8},{8,12},{12,16},{16,20},{20,24},{24,28},{28,0},{1,5},{5... | collective-permute-start | bytes 62216 | tf_op jit(solution)/shard_map/while/body/eval_jaxpr/ppermute | solution.py:13
  493.2 12.5 %collective-permute-start.4 = (f32[81,64]{0,1:T(8,128)S(1)}, f32[81,64]{0,1:T(8,128)S(1)}, u32[]{:S(2)}, u32[]{:S(2)}) collective-permute-start(f32[81,64]{0,1:T(8,128)S(1)} %maximum_select_fusion.2), channel_id=1, source_target_pairs={{0,28},{4,0},{8,4},{12,8},{16,12},{20,16},{24,20},{28,24},{1,29},{... | collective-permute-start | bytes 62216 | tf_op jit(solution)/shard_map/while/body/eval_jaxpr/ppermute | solution.py:13
  496.0 9.7 %collective-permute-start.3 = (f32[81,64]{0,1:T(8,128)S(1)}, f32[81,64]{0,1:T(8,128)S(1)}, u32[]{:S(2)}, u32[]{:S(2)}) collective-permute-start(f32[81,64]{0,1:T(8,128)S(1)} %maximum_select_fusion.2), channel_id=1, source_target_pairs={{0,8},{4,12},{8,16},{12,20},{16,24},{20,28},{24,0},{28,4},{1,9},{5... | collective-permute-start | bytes 62216 | tf_op jit(solution)/shard_map/while/body/eval_jaxpr/ppermute | solution.py:13
  496.0 9.7 %collective-permute-start.2 = (f32[81,64]{0,1:T(8,128)S(1)}, f32[81,64]{0,1:T(8,128)S(1)}, u32[]{:S(2)}, u32[]{:S(2)}) collective-permute-start(f32[81,64]{0,1:T(8,128)S(1)} %maximum_select_fusion.2), channel_id=1, source_target_pairs={{0,24},{4,28},{8,0},{12,4},{16,8},{20,12},{24,16},{28,20},{1,25},{... | collective-permute-start | bytes 62216 | tf_op jit(solution)/shard_map/while/body/eval_jaxpr/ppermute | solution.py:13
  544.7 8.6 %collective-permute-start.5 = (f32[81,64]{0,1:T(8,128)S(1)}, f32[81,64]{0,1:T(8,128)S(1)}, u32[]{:S(2)}, u32[]{:S(2)}) collective-permute-start(f32[81,64]{0,1:T(8,128)S(1)} %maximum_select_fusion.2), channel_id=1, source_target_pairs={{0,4},{4,8},{8,12},{12,16},{16,20},{20,24},{24,28},{28,0},{1,5},{5... | collective-permute-start | bytes 62216 | tf_op jit(solution)/shard_map/while/body/eval_jaxpr/ppermute | solution.py:13
  545.5 13.6 %collective-permute-start.4 = (f32[81,64]{0,1:T(8,128)S(1)}, f32[81,64]{0,1:T(8,128)S(1)}, u32[]{:S(2)}, u32[]{:S(2)}) collective-permute-start(f32[81,64]{0,1:T(8,128)S(1)} %maximum_select_fusion.2), channel_id=1, source_target_pairs={{0,28},{4,0},{8,4},{12,8},{16,12},{20,16},{24,20},{28,24},{1,29},{... | collective-permute-start | bytes 62216 | tf_op jit(solution)/shard_map/while/body/eval_jaxpr/ppermute | solution.py:13
  549.4 9.7 %collective-permute-start.3 = (f32[81,64]{0,1:T(8,128)S(1)}, f32[81,64]{0,1:T(8,128)S(1)}, u32[]{:S(2)}, u32[]{:S(2)}) collective-permute-start(f32[81,64]{0,1:T(8,128)S(1)} %maximum_select_fusion.2), channel_id=1, source_target_pairs={{0,8},{4,12},{8,16},{12,20},{16,24},{20,28},{24,0},{28,4},{1,9},{5... | collective-permute-start | bytes 62216 | tf_op jit(solution)/shard_map/while/body/eval_jaxpr/ppermute | solution.py:13
  549.4 9.7 %collective-permute-start.2 = (f32[81,64]{0,1:T(8,128)S(1)}, f32[81,64]{0,1:T(8,128)S(1)}, u32[]{:S(2)}, u32[]{:S(2)}) collective-permute-start(f32[81,64]{0,1:T(8,128)S(1)} %maximum_select_fusion.2), channel_id=1, source_target_pairs={{0,24},{4,28},{8,0},{12,4},{16,8},{20,12},{24,16},{28,20},{1,25},{... | collective-permute-start | bytes 62216 | tf_op jit(solution)/shard_map/while/body/eval_jaxpr/ppermute | solution.py:13
  598.5 8.6 %collective-permute-start.5 = (f32[81,64]{0,1:T(8,128)S(1)}, f32[81,64]{0,1:T(8,128)S(1)}, u32[]{:S(2)}, u32[]{:S(2)}) collective-permute-start(f32[81,64]{0,1:T(8,128)S(1)} %maximum_select_fusion.2), channel_id=1, source_target_pairs={{0,4},{4,8},{8,12},{12,16},{16,20},{20,24},{24,28},{28,0},{1,5},{5... | collective-permute-start | bytes 62216 | tf_op jit(solution)/shard_map/while/body/eval_jaxpr/ppermute | solution.py:13
  598.5 14.4 %collective-permute-start.4 = (f32[81,64]{0,1:T(8,128)S(1)}, f32[81,64]{0,1:T(8,128)S(1)}, u32[]{:S(2)}, u32[]{:S(2)}) collective-permute-start(f32[81,64]{0,1:T(8,128)S(1)} %maximum_select_fusion.2), channel_id=1, source_target_pairs={{0,28},{4,0},{8,4},{12,8},{16,12},{20,16},{24,20},{28,24},{1,29},{... | collective-permute-start | bytes 62216 | tf_op jit(solution)/shard_map/while/body/eval_jaxpr/ppermute | solution.py:13
  603.2 9.7 %collective-permute-start.3 = (f32[81,64]{0,1:T(8,128)S(1)}, f32[81,64]{0,1:T(8,128)S(1)}, u32[]{:S(2)}, u32[]{:S(2)}) collective-permute-start(f32[81,64]{0,1:T(8,128)S(1)} %maximum_select_fusion.2), channel_id=1, source_target_pairs={{0,8},{4,12},{8,16},{12,20},{16,24},{20,28},{24,0},{28,4},{1,9},{5... | collective-permute-start | bytes 62216 | tf_op jit(solution)/shard_map/while/body/eval_jaxpr/ppermute | solution.py:13
  603.2 9.7 %collective-permute-start.2 = (f32[81,64]{0,1:T(8,128)S(1)}, f32[81,64]{0,1:T(8,128)S(1)}, u32[]{:S(2)}, u32[]{:S(2)}) collective-permute-start(f32[81,64]{0,1:T(8,128)S(1)} %maximum_select_fusion.2), channel_id=1, source_target_pairs={{0,24},{4,28},{8,0},{12,4},{16,8},{20,12},{24,16},{28,20},{1,25},{... | collective-permute-start | bytes 62216 | tf_op jit(solution)/shard_map/while/body/eval_jaxpr/ppermute | solution.py:13
  646.4 11.7 %collective-permute-start.5 = (f32[81,64]{0,1:T(8,128)S(1)}, f32[81,64]{0,1:T(8,128)S(1)}, u32[]{:S(2)}, u32[]{:S(2)}) collective-permute-start(f32[81,64]{0,1:T(8,128)S(1)} %maximum_select_fusion.2), channel_id=1, source_target_pairs={{0,4},{4,8},{8,12},{12,16},{16,20},{20,24},{24,28},{28,0},{1,5},{5... | collective-permute-start | bytes 62216 | tf_op jit(solution)/shard_map/while/body/eval_jaxpr/ppermute | solution.py:13
  650.9 12.0 %collective-permute-start.4 = (f32[81,64]{0,1:T(8,128)S(1)}, f32[81,64]{0,1:T(8,128)S(1)}, u32[]{:S(2)}, u32[]{:S(2)}) collective-permute-start(f32[81,64]{0,1:T(8,128)S(1)} %maximum_select_fusion.2), channel_id=1, source_target_pairs={{0,28},{4,0},{8,4},{12,8},{16,12},{20,16},{24,20},{28,24},{1,29},{... | collective-permute-start | bytes 62216 | tf_op jit(solution)/shard_map/while/body/eval_jaxpr/ppermute | solution.py:13
  653.2 9.7 %collective-permute-start.3 = (f32[81,64]{0,1:T(8,128)S(1)}, f32[81,64]{0,1:T(8,128)S(1)}, u32[]{:S(2)}, u32[]{:S(2)}) collective-permute-start(f32[81,64]{0,1:T(8,128)S(1)} %maximum_select_fusion.2), channel_id=1, source_target_pairs={{0,8},{4,12},{8,16},{12,20},{16,24},{20,28},{24,0},{28,4},{1,9},{5... | collective-permute-start | bytes 62216 | tf_op jit(solution)/shard_map/while/body/eval_jaxpr/ppermute | solution.py:13
  655.5 7.5 collective-permute-start.2
  702.7 8.6 %collective-permute-start.5 = (f32[81,64]{0,1:T(8,128)S(1)}, f32[81,64]{0,1:T(8,128)S(1)}, u32[]{:S(2)}, u32[]{:S(2)}) collective-permute-start(f32[81,64]{0,1:T(8,128)S(1)} %maximum_select_fusion.2), channel_id=1, source_target_pairs={{0,4},{4,8},{8,12},{12,16},{16,20},{20,24},{24,28},{28,0},{1,5},{5... | collective-permute-start | bytes 62216 | tf_op jit(solution)/shard_map/while/body/eval_jaxpr/ppermute | solution.py:13
  704.7 12.4 %collective-permute-start.4 = (f32[81,64]{0,1:T(8,128)S(1)}, f32[81,64]{0,1:T(8,128)S(1)}, u32[]{:S(2)}, u32[]{:S(2)}) collective-permute-start(f32[81,64]{0,1:T(8,128)S(1)} %maximum_select_fusion.2), channel_id=1, source_target_pairs={{0,28},{4,0},{8,4},{12,8},{16,12},{20,16},{24,20},{28,24},{1,29},{... | collective-permute-start | bytes 62216 | tf_op jit(solution)/shard_map/while/body/eval_jaxpr/ppermute | solution.py:13
  707.4 9.7 %collective-permute-start.3 = (f32[81,64]{0,1:T(8,128)S(1)}, f32[81,64]{0,1:T(8,128)S(1)}, u32[]{:S(2)}, u32[]{:S(2)}) collective-permute-start(f32[81,64]{0,1:T(8,128)S(1)} %maximum_select_fusion.2), channel_id=1, source_target_pairs={{0,8},{4,12},{8,16},{12,20},{16,24},{20,28},{24,0},{28,4},{1,9},{5... | collective-permute-start | bytes 62216 | tf_op jit(solution)/shard_map/while/body/eval_jaxpr/ppermute | solution.py:13
  707.4 9.7 %collective-permute-start.2 = (f32[81,64]{0,1:T(8,128)S(1)}, f32[81,64]{0,1:T(8,128)S(1)}, u32[]{:S(2)}, u32[]{:S(2)}) collective-permute-start(f32[81,64]{0,1:T(8,128)S(1)} %maximum_select_fusion.2), channel_id=1, source_target_pairs={{0,24},{4,28},{8,0},{12,4},{16,8},{20,12},{24,16},{28,20},{1,25},{... | collective-permute-start | bytes 62216 | tf_op jit(solution)/shard_map/while/body/eval_jaxpr/ppermute | solution.py:13
  756.0 8.6 %collective-permute-start.5 = (f32[81,64]{0,1:T(8,128)S(1)}, f32[81,64]{0,1:T(8,128)S(1)}, u32[]{:S(2)}, u32[]{:S(2)}) collective-permute-start(f32[81,64]{0,1:T(8,128)S(1)} %maximum_select_fusion.2), channel_id=1, source_target_pairs={{0,4},{4,8},{8,12},{12,16},{16,20},{20,24},{24,28},{28,0},{1,5},{5... | collective-permute-start | bytes 62216 | tf_op jit(solution)/shard_map/while/body/eval_jaxpr/ppermute | solution.py:13
  756.8 13.7 %collective-permute-start.4 = (f32[81,64]{0,1:T(8,128)S(1)}, f32[81,64]{0,1:T(8,128)S(1)}, u32[]{:S(2)}, u32[]{:S(2)}) collective-permute-start(f32[81,64]{0,1:T(8,128)S(1)} %maximum_select_fusion.2), channel_id=1, source_target_pairs={{0,28},{4,0},{8,4},{12,8},{16,12},{20,16},{24,20},{28,24},{1,29},{... | collective-permute-start | bytes 62216 | tf_op jit(solution)/shard_map/while/body/eval_jaxpr/ppermute | solution.py:13
  760.8 9.7 %collective-permute-start.3 = (f32[81,64]{0,1:T(8,128)S(1)}, f32[81,64]{0,1:T(8,128)S(1)}, u32[]{:S(2)}, u32[]{:S(2)}) collective-permute-start(f32[81,64]{0,1:T(8,128)S(1)} %maximum_select_fusion.2), channel_id=1, source_target_pairs={{0,8},{4,12},{8,16},{12,20},{16,24},{20,28},{24,0},{28,4},{1,9},{5... | collective-permute-start | bytes 62216 | tf_op jit(solution)/shard_map/while/body/eval_jaxpr/ppermute | solution.py:13
  760.8 9.7 %collective-permute-start.2 = (f32[81,64]{0,1:T(8,128)S(1)}, f32[81,64]{0,1:T(8,128)S(1)}, u32[]{:S(2)}, u32[]{:S(2)}) collective-permute-start(f32[81,64]{0,1:T(8,128)S(1)} %maximum_select_fusion.2), channel_id=1, source_target_pairs={{0,24},{4,28},{8,0},{12,4},{16,8},{20,12},{24,16},{28,20},{1,25},{... | collective-permute-start | bytes 62216 | tf_op jit(solution)/shard_map/while/body/eval_jaxpr/ppermute | solution.py:13
  804.5 11.7 %collective-permute-start.5 = (f32[81,64]{0,1:T(8,128)S(1)}, f32[81,64]{0,1:T(8,128)S(1)}, u32[]{:S(2)}, u32[]{:S(2)}) collective-permute-start(f32[81,64]{0,1:T(8,128)S(1)} %maximum_select_fusion.2), channel_id=1, source_target_pairs={{0,4},{4,8},{8,12},{12,16},{16,20},{20,24},{24,28},{28,0},{1,5},{5... | collective-permute-start | bytes 62216 | tf_op jit(solution)/shard_map/while/body/eval_jaxpr/ppermute | solution.py:13
  809.8 11.1 %collective-permute-start.4 = (f32[81,64]{0,1:T(8,128)S(1)}, f32[81,64]{0,1:T(8,128)S(1)}, u32[]{:S(2)}, u32[]{:S(2)}) collective-permute-start(f32[81,64]{0,1:T(8,128)S(1)} %maximum_select_fusion.2), channel_id=1, source_target_pairs={{0,28},{4,0},{8,4},{12,8},{16,12},{20,16},{24,20},{28,24},{1,29},{... | collective-permute-start | bytes 62216 | tf_op jit(solution)/shard_map/while/body/eval_jaxpr/ppermute | solution.py:13
  811.2 9.7 %collective-permute-start.3 = (f32[81,64]{0,1:T(8,128)S(1)}, f32[81,64]{0,1:T(8,128)S(1)}, u32[]{:S(2)}, u32[]{:S(2)}) collective-permute-start(f32[81,64]{0,1:T(8,128)S(1)} %maximum_select_fusion.2), channel_id=1, source_target_pairs={{0,8},{4,12},{8,16},{12,20},{16,24},{20,28},{24,0},{28,4},{1,9},{5... | collective-permute-start | bytes 62216 | tf_op jit(solution)/shard_map/while/body/eval_jaxpr/ppermute | solution.py:13
  813.5 7.5 collective-permute-start.2
  (49 other events, 538.5 us)
where the time goes:
time: 862 us; the launch traced here: 853 us
  blocking collectives  365 us (42%)
  starting transfers between devices  211 us (24%)
  local copies, waits for them, and re-layouts  113 us (13%)
  matrix products  85.5 us (10%)
  loops' own time  68.8 us (8%)
    ppermute x96, starting transfers between devices, shifted(): return lax.ppermute(value, axis, pairs)  211 us
    while x16, blocking collectives  102 us
    all_gather x16, blocking collectives, assimilate(): lax.all_gather(innovation, 'gy', axis=0, tiled=True)  90.1 us
    all_gather x16, blocking collectives, assimilate(): lax.all_gather(weighted, 'gy', axis=1, tiled=True)  86.7 us
    all_gather x16, blocking collectives, assimilate(): lax.all_gather(picked, 'gy', axis=1, tiled=True)  86.4 us
    dot_general x56, matrix products, product(): jnp.dot(left_side, right_side, precision=lax.Precision.HIGHEST, preferred...  85.5 us
    another operation x1, loops' own time, local(): lax.fori_loop(0, BATCHES, assimilate, (start_rows, start_mean))  60.8 us
    while x128, local copies, waits for them, and re-layouts  22.2 us
  transfers between devices with their start and end apart: 96, of which 6 were waited for; matrix products, arithmetic and copies ran while one was open for 1% of the time, Pallas kernels for 0%

commit v1 on v0

v1 whole, which is shorter than its diff:
```python
import functools

import jax
import jax.numpy as jnp
from jax import lax
from jax.experimental import pallas as pl
from jax.experimental.pallas import tpu as pltpu
from jax.sharding import PartitionSpec as P

REACH = 3
LANES = 128
MESH = pl.DeviceIdType.MESH
VMEM = pl.BlockSpec(memory_space=pltpu.VMEM)
SMEM = pl.BlockSpec(memory_space=pltpu.SMEM)
F32 = jnp.float32
BF16 = jnp.bfloat16


def split(value):
    high = value.astype(BF16)
    return high, (value - high.astype(F32)).astype(BF16)


def nn(left, right):
    return lax.dot_general(left, right, (((1,), (0,)), ((), ())), preferred_element_type=F32)


def nt(left, right):
    return lax.dot_general(left, right, (((1,), (1,)), ((), ())), preferred_element_type=F32)


def lane_ids(shape):
    return lax.broadcasted_iota(jnp.int32, shape, len(shape) - 1)


def pick_kernel(lon_dev, lat_dev, cells_ref, value_ref, owned_ref, anom_ref, mean_ref, state_ref, rows_ref):
    column, band = lax.axis_index("gx"), lax.axis_index("gy")
    members, classes, levels = anom_ref.shape
    batches, quarter = value_ref.shape

    for c in range(classes):
        lat = (band * lat_dev + c % lat_dev).astype(F32)
        lon = (column * lon_dev + c // lat_dev).astype(F32)
        tall = jnp.concatenate(
            [
                anom_ref[:, c, :],
                mean_ref[pl.ds(c, 1), :],
                jnp.full((1, levels), lat, F32),
                jnp.full((1, levels), lon, F32),
                jnp.zeros((LANES - members - 3, levels), F32),
            ],
            axis=0,
        )
        state_ref[pl.ds(c * levels, levels), :] = tall.T

    lane = lane_ids((1, LANES))

    def batch(t, _):
        mine = owned_ref[t] == column

        @pl.when(mine)
        def _():
            def group(i, _):
                for k in range(8):
                    j = i * 8 + k
                    row = state_ref[pl.ds(cells_ref[t, j], 1), :]
                    rows_ref[pl.ds(t * quarter + j, 1), :] = jnp.where(lane == members + 3, value_ref[t, j], row)
                return 0

            lax.fori_loop(0, quarter // 8, group, 0)

        @pl.when(jnp.logical_not(mine))
        def _():
            rows_ref[pl.ds(pl.multiple_of(t * quarter, quarter), quarter), :] = jnp.zeros((quarter, LANES), F32)

        return 0

    lax.fori_loop(0, batches, batch, 0)


def main_kernel(
    sizes, order_ref, state_ref, obs_ref, lat_ref, lon_ref, root_ref, gain_ref,
    anom_out, mean_out,
    cells_s, obs_s, v_s, vw_s, z3_s, gh_s, gl_s, send_sem, recv_sem,
):
    members, lon_dev, lat_dev, levels, lon_total, lat_total, span, bands = sizes
    batches, _, obs = lat_ref.shape
    quarter = obs // bands
    column, band = lax.axis_index("gx"), lax.axis_index("gy")
    classes = lon_dev * lat_dev
    chunk = 4

    barrier = pltpu.get_barrier_semaphore()
    for k in range(1, bands):
        pl.semaphore_signal(barrier, inc=1, device_id={"gy": lax.rem(band + k, bands)}, device_id_type=MESH)
    pl.semaphore_wait(barrier, bands - 1)

    def widen(value, with_low_in_middle):
        high, low = split(value)
        high, low = high.astype(F32), low.astype(F32)
        second, third = (low, high) if with_low_in_middle else (high, low)
        lane = lane_ids(value.shape)
        room = LANES - members
        moved = pltpu.roll(second, members, 1)
        first = jnp.where(lane < members, high, moved)
        last = jnp.where(lane < members - room, moved, pltpu.roll(third, members - room, 1))
        return jnp.concatenate([first, last], axis=1), lane, room

    def state_wide(value):
        return widen(value, True)[0].astype(BF16)

    def prior_wide(value):
        wide, lane, room = widen(jnp.where(lane_ids(value.shape) < members, value, 0.0), False)
        wide_lane = lane_ids(wide.shape)
        return jnp.where(wide_lane < 3 * members, wide, 0.0).astype(BF16)

    def lon_weight(gap):
        gap = jnp.abs(gap)
        gap = jnp.minimum(gap, lon_total - gap)
        return jnp.maximum(0.0, 1.0 - gap * (1.0 / span))

    def lat_weight(gap):
        return 1.0 - jnp.abs(gap) * (1.0 / lat_total)

    def obs_taper(rows, s):
        lat, lon = rows[:, members + 1:members + 2], rows[:, members + 2:members + 3]
        return lat_weight(lat - lat_ref[s]) * lon_weight(lon - lon_ref[s])

    def apply(rows, high, low):
        both = nn(high, vw_s[...])
        return rows - (both[:, :LANES] + both[:, LANES:] + nn(low, vw_s[:, :LANES]))

    def update(rows, taper, s):
        gained = nt(state_wide(rows), z3_s[lax.rem(s, 2)]) * taper
        return apply(rows, *split(gained))

    def update_cells(source_ref, s):
        def some(i, _):
            tapers = []
            for k in range(chunk):
                c = i * chunk + k
                lat = (band * lat_dev + lax.rem(c, lat_dev)).astype(F32)
                lon = (column * lon_dev + c // lat_dev).astype(F32)
                weight = lat_weight(lat - lat_ref[s]) * lon_weight(lon - lon_ref[s])
                tapers.append(jnp.broadcast_to(weight, (levels, obs)))
            here = pl.ds(pl.multiple_of(i * (chunk * levels), chunk * levels), chunk * levels)
            cells_s[here, :] = update(source_ref[here, :], jnp.concatenate(tapers, axis=0), s)
            return 0

        lax.fori_loop(0, classes // chunk, some, 0)

    def at(t):
        return pl.ds(pl.multiple_of(t * obs, obs), obs)

    cells_s[...] = state_ref[...]
    obs_s[...] = obs_ref[...]

    def turn(t, _):
        prior = obs_s[at(t), :]
        lane = lane_ids(prior.shape)
        innovation = pltpu.roll(prior, LANES - 3, 1) - prior
        joined = jnp.where(lane < members, prior, jnp.where(lane == members, innovation, 0.0))
        high, low = split(joined)
        batch_id = order_ref[t]
        table_high, table_low = split(jnp.concatenate([root_ref[batch_id], gain_ref[batch_id]], axis=0))
        both = nn(table_high, jnp.concatenate([high, low], axis=1))
        part = both[:, :LANES] + both[:, LANES:] + nn(table_low, high)
        lane = lane_ids((quarter, LANES))
        weighted = jnp.where(lane < members, part[:quarter], jnp.where(lane == members, -part[quarter:], 0.0))
        mine = pl.ds(pl.multiple_of(band * quarter, quarter), quarter)
        v_s[t, mine, :] = weighted * (1.0 / (members - 1.0))

        def copy(k):
            return pltpu.make_async_remote_copy(
                src_ref=v_s.at[t, mine, :],
                dst_ref=v_s.at[t, mine, :],
                send_sem=send_sem.at[t, k - 1],
                recv_sem=recv_sem.at[t, k - 1],
                device_id={"gy": lax.rem(band + k, bands)},
                device_id_type=MESH,
            )

        for k in range(1, bands):
            copy(k).start()

        z3_s[lax.rem(t, 2)] = prior_wide(prior)

        @pl.when(t < batches - 1)
        def _():
            rows = obs_s[at(t + 1), :]

            @pl.when(t > 0)
            def _():
                obs_s[at(t + 1), :] = update(rows, obs_taper(rows, t - 1), t - 1)

            rows = obs_s[at(t + 1), :]
            gained = nt(state_wide(rows), z3_s[lax.rem(t, 2)]) * obs_taper(rows, t)
            gh_s[...], gl_s[...] = split(gained)

        @pl.when(t > 0)
        def _():
            def later(n, _):
                rows = obs_s[at(n), :]
                obs_s[at(n), :] = update(rows, obs_taper(rows, t - 1), t - 1)
                return 0

            lax.fori_loop(t + 2, batches, later, 0)
            update_cells(cells_s, t - 1)

        for k in range(1, bands):
            copy(k).wait()

        vw_s[...] = jnp.concatenate(split(v_s[t]), axis=1)

        @pl.when(t < batches - 1)
        def _():
            obs_s[at(t + 1), :] = apply(obs_s[at(t + 1), :], gh_s[...], gl_s[...])

        return 0

    lax.fori_loop(0, batches, turn, 0)
    update_cells(cells_s, batches - 1)
    for c in range(classes):
        tall = cells_s[pl.ds(c * levels, levels), :].T
        anom_out[:, c, :] = tall[:members]
        mean_out[pl.ds(c, 1), :] = tall[members:members + 1]


def local(anomalies, state_mean, obs_value, obs_cell, owner, order, root_inv, gain_inv):
    members, lon_dev, lat_dev, levels = anomalies.shape
    classes = lon_dev * lat_dev
    cells = classes * levels
    batches, quarter = obs_value.shape
    obs = obs_cell.shape[1]
    slabs, bands = lax.axis_size("gx"), lax.axis_size("gy")
    band = lax.axis_index("gy")
    owned = owner[order]
    cells_of = obs_cell[order]
    own_cells = lax.dynamic_slice_in_dim(cells_of, band * quarter, quarter, axis=1)
    own_values = obs_value[order]
    obs_lat = jnp.arange(obs, dtype=jnp.int32)[None, :] // quarter * lat_dev + cells_of // levels % lat_dev
    obs_lon = owned[:, None] * lon_dev + cells_of // (lat_dev * levels)

    state, rows = pl.pallas_call(
        functools.partial(pick_kernel, lon_dev, lat_dev),
        out_shape=(
            jax.ShapeDtypeStruct((cells, LANES), F32),
            jax.ShapeDtypeStruct((batches * quarter, LANES), F32),
        ),
        in_specs=[SMEM, SMEM, SMEM, VMEM, VMEM],
        out_specs=(VMEM, VMEM),
        name="pick",
    )(own_cells, own_values, owned, anomalies.reshape(members, classes, levels), state_mean.reshape(classes, levels))

    rows = lax.psum(rows.reshape(batches, quarter, LANES), "gx")
    rows = lax.all_gather(rows, "gy", axis=1, tiled=True).reshape(batches * obs, LANES)

    sizes = (
        members, lon_dev, lat_dev, levels, float(slabs * lon_dev), float(bands * lat_dev), REACH * lon_dev + 1.0, bands
    )
    post, mean = pl.pallas_call(
        functools.partial(main_kernel, sizes),
        out_shape=(
            jax.ShapeDtypeStruct((members, classes, levels), F32),
            jax.ShapeDtypeStruct((classes, levels), F32),
        ),
        in_specs=[SMEM] + [VMEM] * 6,
        out_specs=(VMEM, VMEM),
        scratch_shapes=[
            pltpu.VMEM((cells, LANES), F32),
            pltpu.VMEM((batches * obs, LANES), F32),
            pltpu.VMEM((batches, obs, LANES), F32),
            pltpu.VMEM((obs, 2 * LANES), BF16),
            pltpu.VMEM((2, obs, 2 * LANES), BF16),
            pltpu.VMEM((obs, obs), BF16),
            pltpu.VMEM((obs, obs), BF16),
            pltpu.SemaphoreType.DMA((batches, bands - 1)),
            pltpu.SemaphoreType.DMA((batches, bands - 1)),
        ],
        compiler_params=pltpu.CompilerParams(collective_id=0, has_side_effects=True),
        name="analysis",
    )(
        order, state, rows, obs_lat.astype(F32)[:, None, :], obs_lon.astype(F32)[:, None, :], root_inv, gain_inv,
    )
    return post.reshape(members, lon_dev, lat_dev, levels), mean.reshape(lon_dev, lat_dev, levels)


def solution(mesh):
    return jax.shard_map(
        local,
        mesh=mesh,
        in_specs=(
            P(None, "gx", "gy", None),
            P("gx", "gy", None),
            P(None, "gy"),
            P(),
            P(),
            P(),
            P(None, "gy", None),
            P(None, "gy", None),
        ),
        out_specs=(P(None, "gx", "gy", None), P("gx", "gy", None)),
        check_vma=False,
    )
```

time: 862 us -> 233 us (0.27)
  blocking collectives: 365 us -> 0 us
  starting transfers between devices: 211 us -> 0.08 us
  Pallas kernels: 0 us -> 111 us
  local copies, waits for them, and re-layouts: 113 us -> 8.24 us
  waiting for transfers between devices: 1.49 us -> 97.1 us
  matrix products: 85.5 us -> 0 us
  loops' own time: 68.8 us -> 0 us
  between operations: 0.65 us -> 14.1 us
    all_gather x48 -> x0, blocking collectives: 263 us -> none  [the longest x16 90.1 us: assimilate(): lax.all_gather(innovation, 'gy', axis=0, tiled=True)]
    ppermute x96 -> x0, starting transfers between devices: 211 us -> none  [shifted(): return lax.ppermute(value, axis, pairs)]
    pallas_call x0 -> x2, Pallas kernels: none -> 111 us  [the longest x1 107 us: local(): pl.pallas_call(functools.partial(main_kernel, sizes), out_shape=(jax.Shap...]
    while x16 -> x0, blocking collectives: 102 us -> none
    dot_general x56 -> x0, matrix products: 85.5 us -> none  [product(): jnp.dot(left_side, right_side, precision=lax.Precision.HIGHEST, preferred...]
    psum x0 -> x1, waiting for transfers between devices: none -> 75.2 us  [local(): rows = lax.psum(rows.reshape(batches, quarter, LANES), 'gx')]
    another operation x17 -> x0, loops' own time: 68.8 us -> none  [the longest x1 60.8 us: local(): lax.fori_loop(0, BATCHES, assimilate, (start_rows, start_mean))]
    dynamic_slice x96 -> x1, local copies, waits for them, and re-layouts: 59.2 us -> 0.68 us  [local(): lax.dynamic_slice_in_dim(cells_of, band * quarter, quarter, axis=1)]
  transfers between devices with their start and end apart: 96 -> 2, of which waited for: 6 -> 2; matrix products, arithmetic and copies ran while one was open for 1% -> 1% of each run, Pallas kernels for 0% -> 0%
where the time goes in v1:
time: 233 us; the launch traced here: 232 us
  Pallas kernels  111 us (48%)
  waiting for transfers between devices  97.1 us (42%)
  between operations  14.1 us (6%)
  local copies, waits for them, and re-layouts  8.24 us (4%)
    pallas_call x1, Pallas kernels, local(): pl.pallas_call(functools.partial(main_kernel, sizes), out_shape=(jax.Shap...  107 us
    psum x1, waiting for transfers between devices, local(): rows = lax.psum(rows.reshape(batches, quarter, LANES), 'gx')  75.2 us
    all_gather x1, waiting for transfers between devices, local(): lax.all_gather(rows, 'gy', axis=1, tiled=True).reshape(batches * obs, LANES)  21.8 us
  transfers between devices with their start and end apart: 2, of which 2 were waited for; matrix products, arithmetic and copies ran while one was open for 1% of the time, Pallas kernels for 0%

profile of v1, /device:TPU:0, one launch (start us, length us, event | category | flops | bytes accessed | tf_op | source)
XLA Modules:
  0.0 232.4 jit_solution(2776386871949494314)
XLA Ops:
  7.2 0.0 copy-start
  7.2 0.0 all-reduce.2.cloned.1.call-start
  7.2 0.7 compare_select_fusion.2
  7.9 1.9 gather_fusion.2
  9.8 1.8 gather_fusion.1
  11.6 0.0 copy-done
  11.6 0.6 gather_fusion
  12.2 0.7 constant_dynamic-slice_fusion.cells_ref
  12.9 3.4 %pick.1 = (f32[2048,128]{1,0:T(8,128)}, f32[1024,128]{1,0:T(8,128)}) custom-call(s32[16,64]{1,0:T(8,128)} %constant_dynamic-slice_fusion.cells_ref, f32[16,64]{1,0:T(8,128)} %gather_fusion.1, s32[16]{0:T(128)} %gather_fusion.2, f32[80,16,128]{2,1,0:T(8,128)} %bitcast.7, f32[16,128]{1,0:T(8,128)} %bitcast.10), custom_call_target="tpu_custom_call" | custom-call | tf_op jit(solution)/shard_map/pick/pallas_call | solution.py:244
  16.2 0.0 all-reduce.2.cloned.1.call-update
  16.3 0.0 all-gather.2.cloned.1.call-start
  16.3 75.2 %all-reduce.2.cloned.1.call-done = f32[16,64,128]{2,1,0:T(8,128)} async-done(((f32[16,64,128]{2,1,0:T(8,128)}), f32[16,64,128]{2,1,0:T(8,128)}) %all-reduce.2.cloned.1.call-update) | async-done | bytes 524304 | tf_op jit(solution)/shard_map/psum | solution.py:255
  91.5 0.0 all-gather.2.cloned.1.call-update
  91.6 0.7 broadcast_multiply_fusion
  92.2 0.8 add_convert_fusion
  93.0 21.8 %all-gather.2.cloned.1.call-done = f32[16,256,128]{2,1,0:T(8,128)} async-done(((f32[16,64,128]{2,1,0:T(8,128)}), f32[16,256,128]{2,1,0:T(8,128)}) %all-gather.2.cloned.1.call-update) | async-done | bytes 2097168 | tf_op jit(solution)/shard_map/all_gather | solution.py:256
  114.9 107.4 %analysis.1 = (f32[80,16,128]{2,1,0:T(8,128)}, f32[16,128]{1,0:T(8,128)}) custom-call(s32[16]{0:T(128)} %order_ref.1, f32[2048,128]{1,0:T(8,128)} %get-tuple-element.6.state_ref, f32[4096,128]{1,0:T(8,128)} %bitcast.6, f32[16,1,256]{2,1,0:T(1,128)} %get-tuple-element.11.lat_ref, f32[16,1,256]{2,1,0:T(1,128)} %get-tuple-element.10.lon_ref, ...), custom_call_target="tpu_custom_call" | custom-call | tf_op jit(solution)/shard_map/analysis/pallas_call | solution.py:261
  222.3 2.0 copy.13
  224.3 1.3 copy.14
  (2 shorter events, 0.0 us)
Async XLA Ops:
  7.2 4.5 %copy-start = (s32[16,256]{1,0:T(8,128)S(1)}, s32[16,256]{1,0:T(8,128)}, u32[]{:S(2)}) copy-start(s32[16,256]{1,0:T(8,128)} %param.11) | copy-start | bytes 49156
  7.2 84.3 %all-reduce.2.cloned.1.call-start = ((), (), s32[]{:S(2)}) async-start(), calls=%async_computation | async-start | bytes 1048576 | tf_op jit(solution)/shard_map/psum | solution.py:255
  16.3 98.6 %all-gather.2.cloned.1.call-start = ((), (), s32[]{:S(2)}) async-start(), calls=%async_computation.1 | async-start | bytes 2621440 | tf_op jit(solution)/shard_map/all_gather | solution.py:256
Sparse Core Ops, SparseCore 0:
  16.4 75.0 all-reduce.1
  93.1 21.7 all-gather.1

commit v2 on v1

--- a/solution.py
+++ b/solution.py
@@ -33,7 +33,7 @@
     return lax.broadcasted_iota(jnp.int32, shape, len(shape) - 1)
 
 
-def pick_kernel(lon_dev, lat_dev, cells_ref, value_ref, owned_ref, anom_ref, mean_ref, state_ref, rows_ref):
+def pick_kernel(lon_dev, lat_dev, cells_ref, value_ref, owner_ref, order_ref, anom_ref, mean_ref, state_ref, rows_ref):
     column, band = lax.axis_index("gx"), lax.axis_index("gy")
     members, classes, levels = anom_ref.shape
     batches, quarter = value_ref.shape
@@ -56,15 +56,16 @@
     lane = lane_ids((1, LANES))
 
     def batch(t, _):
-        mine = owned_ref[t] == column
+        b = order_ref[t]
+        mine = owner_ref[b] == column
 
         @pl.when(mine)
         def _():
             def group(i, _):
                 for k in range(8):
                     j = i * 8 + k
-                    row = state_ref[pl.ds(cells_ref[t, j], 1), :]
-                    rows_ref[pl.ds(t * quarter + j, 1), :] = jnp.where(lane == members + 3, value_ref[t, j], row)
+                    row = state_ref[pl.ds(cells_ref[b, band * quarter + j], 1), :]
+                    rows_ref[pl.ds(t * quarter + j, 1), :] = jnp.where(lane == members + 3, value_ref[b, j], row)
                 return 0
 
             lax.fori_loop(0, quarter // 8, group, 0)
@@ -78,13 +79,106 @@
     lax.fori_loop(0, batches, batch, 0)
 
 
+def spread_kernel(bands, slabs, rows_ref, out_ref, land, send1, recv1, send2, recv2, send3, recv3, send4, recv4, send5, recv5):
+    x, b = lax.axis_index("gx"), lax.axis_index("gy")
+    partner = b + 1 - 2 * lax.rem(b, 2)
+    across = lax.rem(b + 2, bands)
+    chunk = land.shape[1]
+
+    def piece(q):
+        return pl.ds(pl.multiple_of(q * chunk, chunk), chunk)
+
+    def slab(k):
+        return lax.rem(x + k, slabs)
+
+    def source(k):
+        return lax.rem(x + slabs - k, slabs)
+
+    def first(k):
+        return pltpu.make_async_remote_copy(
+            src_ref=rows_ref.at[piece(slab(k)), :], dst_ref=land.at[k], send_sem=send1.at[k], recv_sem=recv1.at[k],
+            device_id={"gx": slab(k)}, device_id_type=MESH,
+        )
+
+    def second(k):
+        return pltpu.make_async_remote_copy(
+            src_ref=out_ref.at[b, piece(x), :], dst_ref=out_ref.at[b, piece(x), :], send_sem=send2.at[k],
+            recv_sem=recv2.at[k], device_id={"gx": slab(k)}, device_id_type=MESH,
+        )
+
+    def hand(k, of_band, send_sem, recv_sem, target):
+        place = out_ref.at[of_band, piece(source(k)), :]
+        return pltpu.make_async_remote_copy(
+            src_ref=place, dst_ref=place, send_sem=send_sem.at[k], recv_sem=recv_sem.at[k],
+            device_id={"gy": target}, device_id_type=MESH,
+        )
+
+    def third(k):
+        return hand(k, b, send3, recv3, partner)
+
+    def fourth(k):
+        return hand(k, b, send4, recv4, across)
+
+    def fifth(k):
+        return hand(k, across, send5, recv5, partner)
+
+    def each(low, high, body):
+        def step(k, _):
+            body(k)
+            return 0
+
+        lax.fori_loop(low, high, step, 0)
+
+    barrier = pltpu.get_barrier_semaphore()
+    each(1, slabs, lambda k: pl.semaphore_signal(barrier, inc=1, device_id={"gx": slab(k)}, device_id_type=MESH))
+    for target in (partner, across):
+        pl.semaphore_signal(barrier, inc=1, device_id={"gy": target}, device_id_type=MESH)
+    pl.semaphore_wait(barrier, slabs + 1)
+
+    each(1, slabs, lambda k: first(k).start())
+    out_ref[b, piece(x), :] = rows_ref[piece(x), :]
+
+    def add(k):
+        first(k).wait_recv()
+        out_ref[b, piece(x), :] += land[k]
+
+    each(1, slabs, add)
+    fourth(0).start()
+    each(1, slabs, lambda k: second(k).start())
+    third(0).start()
+
+    def relay(k):
+        second(k).wait_recv()
+        fourth(k).start()
+        third(k).start()
+        fourth(k - 1).wait_recv()
+        fifth(k - 1).start()
+
+    each(1, slabs, relay)
+    fourth(slabs - 1).wait_recv()
+    fifth(slabs - 1).start()
+
+    def finish(k):
+        third(k).wait()
+        fifth(k).wait()
+        fourth(k).wait_send()
+
+    each(0, slabs, finish)
+
+    def sent(k):
+        first(k).wait_send()
+        second(k).wait_send()
+
+    each(1, slabs, sent)
+
+
 def main_kernel(
-    sizes, order_ref, state_ref, obs_ref, lat_ref, lon_ref, root_ref, gain_ref,
+    sizes, order_ref, owner_ref, state_ref, obs_ref, cell_ref, root_ref, gain_ref,
     anom_out, mean_out,
-    cells_s, obs_s, v_s, vw_s, z3_s, gh_s, gl_s, send_sem, recv_sem,
+    lat_ref, lon_ref, cells_s, obs_s, v_s, vw_s, z3_s, gh_s, gl_s, send_sem, recv_sem,
 ):
     members, lon_dev, lat_dev, levels, lon_total, lat_total, span, bands = sizes
-    batches, _, obs = lat_ref.shape
+    batches, obs = cell_ref.shape
     quarter = obs // bands
     column, band = lax.axis_index("gx"), lax.axis_index("gy")
     classes = lon_dev * lat_dev
@@ -130,30 +224,40 @@
         both = nn(high, vw_s[...])
         return rows - (both[:, :LANES] + both[:, LANES:] + nn(low, vw_s[:, :LANES]))
 
-    def update(rows, taper, s):
-        gained = nt(state_wide(rows), z3_s[lax.rem(s, 2)]) * taper
+    def update(rows, taper, s, slot):
+        gained = nt(state_wide(rows), z3_s[slot]) * taper
         return apply(rows, *split(gained))
 
-    def update_cells(source_ref, s):
-        def some(i, _):
+    def update_cells(s, slot):
+        for i in range(classes // chunk):
             tapers = []
             for k in range(chunk):
                 c = i * chunk + k
-                lat = (band * lat_dev + lax.rem(c, lat_dev)).astype(F32)
+                lat = (band * lat_dev + c % lat_dev).astype(F32)
                 lon = (column * lon_dev + c // lat_dev).astype(F32)
                 weight = lat_weight(lat - lat_ref[s]) * lon_weight(lon - lon_ref[s])
                 tapers.append(jnp.broadcast_to(weight, (levels, obs)))
-            here = pl.ds(pl.multiple_of(i * (chunk * levels), chunk * levels), chunk * levels)
-            cells_s[here, :] = update(source_ref[here, :], jnp.concatenate(tapers, axis=0), s)
-            return 0
-
-        lax.fori_loop(0, classes // chunk, some, 0)
+            here = pl.ds(i * chunk * levels, chunk * levels)
+            cells_s[here, :] = update(cells_s[here, :], jnp.concatenate(tapers, axis=0), s, slot)
 
     def at(t):
         return pl.ds(pl.multiple_of(t * obs, obs), obs)
 
     cells_s[...] = state_ref[...]
-    obs_s[...] = obs_ref[...]
+    for t in range(batches):
+        for q in range(bands):
+            obs_s[pl.ds(t * obs + q * quarter, quarter), :] = obs_ref[q, pl.ds(t * quarter, quarter), :]
+    obs_s[pl.ds(batches * obs, 2 * obs), :] = jnp.zeros((2 * obs, LANES), F32)
+    vw_s[...] = jnp.zeros_like(vw_s)
+    z3_s[...] = jnp.zeros_like(z3_s)
+    first_lat = lax.broadcasted_iota(jnp.int32, (1, obs), 1).astype(F32)
+    first_lat = jnp.floor((first_lat + 0.5) * (1.0 / quarter)) * lat_dev
+    for t in range(batches):
+        batch_id = order_ref[t]
+        level_row = jnp.floor((cell_ref[pl.ds(batch_id, 1), :].astype(F32) + 0.5) * (1.0 / levels))
+        lon_row = jnp.floor((level_row + 0.5) * (1.0 / lat_dev))
+        lat_ref[t] = level_row - lon_row * lat_dev + first_lat
+        lon_ref[t] = lon_row + (owner_ref[batch_id] * lon_dev).astype(F32)
 
     def turn(t, _):
         prior = obs_s[at(t), :]
@@ -185,41 +289,33 @@
 
         z3_s[lax.rem(t, 2)] = prior_wide(prior)
 
-        @pl.when(t < batches - 1)
-        def _():
-            rows = obs_s[at(t + 1), :]
-
-            @pl.when(t > 0)
-            def _():
-                obs_s[at(t + 1), :] = update(rows, obs_taper(rows, t - 1), t - 1)
-
-            rows = obs_s[at(t + 1), :]
-            gained = nt(state_wide(rows), z3_s[lax.rem(t, 2)]) * obs_taper(rows, t)
-            gh_s[...], gl_s[...] = split(gained)
-
-        @pl.when(t > 0)
-        def _():
-            def later(n, _):
-                rows = obs_s[at(n), :]
-                obs_s[at(n), :] = update(rows, obs_taper(rows, t - 1), t - 1)
-                return 0
-
-            lax.fori_loop(t + 2, batches, later, 0)
-            update_cells(cells_s, t - 1)
+        before = jnp.maximum(t - 1, 0)
+        past = lax.rem(t + 1, 2)
+        rows = obs_s[at(t + 1), :]
+        rows = update(rows, obs_taper(rows, before), before, past)
+        obs_s[at(t + 1), :] = rows
+        gained = nt(state_wide(rows), z3_s[lax.rem(t, 2)]) * obs_taper(rows, t)
+        gh_s[...], gl_s[...] = split(gained)
+        update_cells(before, past)
+
+        def later(i, _):
+            here = pl.ds(pl.multiple_of((t + 2 + 2 * i) * obs, obs), 2 * obs)
+            rows = obs_s[here, :]
+            obs_s[here, :] = update(rows, obs_taper(rows, before), before, past)
+            return 0
+
+        lax.fori_loop(0, (batches - 1 - t) // 2 * jnp.minimum(t, 1), later, 0)
 
         for k in range(1, bands):
             copy(k).wait()
 
         vw_s[...] = jnp.concatenate(split(v_s[t]), axis=1)
 
-        @pl.when(t < batches - 1)
-        def _():
-            obs_s[at(t + 1), :] = apply(obs_s[at(t + 1), :], gh_s[...], gl_s[...])
-
+        obs_s[at(t + 1), :] = apply(obs_s[at(t + 1), :], gh_s[...], gl_s[...])
         return 0
 
     lax.fori_loop(0, batches, turn, 0)
-    update_cells(cells_s, batches - 1)
+    update_cells(batches - 1, (batches - 1) % 2)
     for c in range(classes):
         tall = cells_s[pl.ds(c * levels, levels), :].T
         anom_out[:, c, :] = tall[:members]
@@ -233,27 +329,30 @@
     batches, quarter = obs_value.shape
     obs = obs_cell.shape[1]
     slabs, bands = lax.axis_size("gx"), lax.axis_size("gy")
-    band = lax.axis_index("gy")
-    owned = owner[order]
-    cells_of = obs_cell[order]
-    own_cells = lax.dynamic_slice_in_dim(cells_of, band * quarter, quarter, axis=1)
-    own_values = obs_value[order]
-    obs_lat = jnp.arange(obs, dtype=jnp.int32)[None, :] // quarter * lat_dev + cells_of // levels % lat_dev
-    obs_lon = owned[:, None] * lon_dev + cells_of // (lat_dev * levels)
-
     state, rows = pl.pallas_call(
         functools.partial(pick_kernel, lon_dev, lat_dev),
         out_shape=(
             jax.ShapeDtypeStruct((cells, LANES), F32),
             jax.ShapeDtypeStruct((batches * quarter, LANES), F32),
         ),
-        in_specs=[SMEM, SMEM, SMEM, VMEM, VMEM],
+        in_specs=[SMEM] * 4 + [VMEM] * 2,
         out_specs=(VMEM, VMEM),
         name="pick",
-    )(own_cells, own_values, owned, anomalies.reshape(members, classes, levels), state_mean.reshape(classes, levels))
-
-    rows = lax.psum(rows.reshape(batches, quarter, LANES), "gx")
-    rows = lax.all_gather(rows, "gy", axis=1, tiled=True).reshape(batches * obs, LANES)
+    )(
+        obs_cell, obs_value, owner, order,
+        anomalies.reshape(members, classes, levels), state_mean.reshape(classes, levels),
+    )
+
+    chunk = batches * quarter // slabs
+    rows = pl.pallas_call(
+        functools.partial(spread_kernel, bands, slabs),
+        out_shape=jax.ShapeDtypeStruct((bands, batches * quarter, LANES), F32),
+        in_specs=[VMEM],
+        out_specs=VMEM,
+        scratch_shapes=[pltpu.VMEM((slabs, chunk, LANES), F32)] + [pltpu.SemaphoreType.DMA((slabs,))] * 10,
+        compiler_params=pltpu.CompilerParams(collective_id=1, has_side_effects=True),
+        name="spread",
+    )(rows)
 
     sizes = (
         members, lon_dev, lat_dev, levels, float(slabs * lon_dev), float(bands * lat_dev), REACH * lon_dev + 1.0, bands
@@ -264,11 +363,13 @@
             jax.ShapeDtypeStruct((members, classes, levels), F32),
             jax.ShapeDtypeStruct((classes, levels), F32),
         ),
-        in_specs=[SMEM] + [VMEM] * 6,
+        in_specs=[SMEM] * 2 + [VMEM] * 5,
         out_specs=(VMEM, VMEM),
         scratch_shapes=[
+            pltpu.VMEM((batches, 1, obs), F32),
+            pltpu.VMEM((batches, 1, obs), F32),
             pltpu.VMEM((cells, LANES), F32),
-            pltpu.VMEM((batches * obs, LANES), F32),
+            pltpu.VMEM(((batches + 2) * obs, LANES), F32),
             pltpu.VMEM((batches, obs, LANES), F32),
             pltpu.VMEM((obs, 2 * LANES), BF16),
             pltpu.VMEM((2, obs, 2 * LANES), BF16),
@@ -280,7 +381,7 @@
         compiler_params=pltpu.CompilerParams(collective_id=0, has_side_effects=True),
         name="analysis",
     )(
-        order, state, rows, obs_lat.astype(F32)[:, None, :], obs_lon.astype(F32)[:, None, :], root_inv, gain_inv,
+        order, owner, state, rows, obs_cell, root_inv, gain_inv,
     )
     return post.reshape(members, lon_dev, lat_dev, levels), mean.reshape(lon_dev, lat_dev, levels)
 

time: 233 us -> 134 us (0.58)
  waiting for transfers between devices: 97.1 us -> 0 us
  Pallas kernels: 111 us -> 129 us
  between operations: 14.1 us -> 0.65 us
  local copies, waits for them, and re-layouts: 8.24 us -> 3.26 us
    psum x1 -> x0, waiting for transfers between devices: 75.2 us -> none  [local(): rows = lax.psum(rows.reshape(batches, quarter, LANES), 'gx')]
    pallas_call x0 -> x1, Pallas kernels: none -> 43 us  [local(): pl.pallas_call(functools.partial(spread_kernel, bands, slabs), out_shape=...]
    pallas_call x1, Pallas kernels: 107 us -> 81.4 us  [local(): pl.pallas_call(functools.partial(main_kernel, sizes), out_shape=(jax.Shap...]
    all_gather x1 -> x0, waiting for transfers between devices: 21.8 us -> none  [local(): lax.all_gather(rows, 'gy', axis=1, tiled=True).reshape(batches * obs, LANES)]
    gather x3 -> x0, local copies, waits for them, and re-layouts: 4.29 us -> none  [the longest x1 1.88 us: local(): owned = owner[order]]
  transfers between devices with their start and end apart: 2 -> 0, of which waited for: 2 -> 0; matrix products, arithmetic and copies ran while one was open for 1% -> 0% of each run, Pallas kernels for 0% -> 0%
where the time goes in v2:
time: 134 us; the launch traced here: 133 us
  Pallas kernels  129 us (96%)
  local copies, waits for them, and re-layouts  3.26 us (2%)
    pallas_call x1, Pallas kernels, local(): pl.pallas_call(functools.partial(main_kernel, sizes), out_shape=(jax.Shap...  81.4 us
    pallas_call x1, Pallas kernels, local(): pl.pallas_call(functools.partial(spread_kernel, bands, slabs), out_shape=...  43 us
    pallas_call x1, Pallas kernels, local(): pl.pallas_call(functools.partial(pick_kernel, lon_dev, lat_dev), out_shap...  4.31 us
    unnamed x2, local copies, waits for them, and re-layouts  3.26 us

profile of v2, /device:TPU:0, one launch (start us, length us, event | category | flops | bytes accessed | tf_op | source)
XLA Modules:
  0.0 132.6 jit_solution(2414187401054423844)
XLA Ops:
  0.6 4.3 %pick.1 = (f32[2048,128]{1,0:T(8,128)}, f32[1024,128]{1,0:T(8,128)}) custom-call(s32[16,256]{1,0:T(8,128)} %cell_ref.1, f32[16,64]{1,0:T(8,128)} %value_ref.1, s32[16]{0:T(128)} %owner_ref.3, s32[16]{0:T(128)} %order_ref.3, f32[80,16,128]{2,1,0:T(8,128)} %bitcast.4, f32[16,128]{1,0:T(8,128)} %bitcast.6), custom_call_target="tpu_custom_call" | custom-call | tf_op jit(solution)/shard_map/pick/pallas_call | solution.py:332
  4.9 43.0 %spread.1.obs_ref = f32[4,1024,128]{2,1,0:T(8,128)} custom-call(f32[1024,128]{1,0:T(8,128)} %get-tuple-element.7.rows_ref), custom_call_target="tpu_custom_call" | custom-call | tf_op jit(solution)/shard_map/spread/pallas_call | solution.py:347
  47.9 81.4 %analysis.1 = (f32[80,16,128]{2,1,0:T(8,128)}, f32[16,128]{1,0:T(8,128)}) custom-call(s32[16]{0:T(128)} %order_ref.3, s32[16]{0:T(128)} %owner_ref.3, f32[2048,128]{1,0:T(8,128)} %get-tuple-element.6.state_ref, f32[4,1024,128]{2,1,0:T(8,128)} %spread.1.obs_ref, s32[16,256]{1,0:T(8,128)} %cell_ref.1, f32[16,64,256]{2,1,0:T(8,128)} %root_ref.1, ...), custom_call_target="tpu_custom_call" | custom-call | tf_op jit(solution)/shard_map/analysis/pallas_call | solution.py:360
  129.3 2.0 %copy.12 = f32[80,2,8,128]{3,2,1,0:T(8,128)} copy(f32[80,2,8,128]{3,2,1,0:T(8,128)} %bitcast.5) | data formatting | bytes 1310720
  131.3 1.3 copy.13

commit v3 on v2

--- a/solution.py
+++ b/solution.py
@@ -33,7 +33,7 @@
     return lax.broadcasted_iota(jnp.int32, shape, len(shape) - 1)
 
 
-def pick_kernel(lon_dev, lat_dev, cells_ref, value_ref, owner_ref, order_ref, anom_ref, mean_ref, state_ref, rows_ref):
+def pick_kernel(lon_dev, lat_dev, cells_ref, value_ref, owner_ref, order_ref, anom_ref, mean_ref, state_ref, packed_ref, rows_ref):
     column, band = lax.axis_index("gx"), lax.axis_index("gy")
     members, classes, levels = anom_ref.shape
     batches, quarter = value_ref.shape
@@ -77,16 +77,15 @@
         return 0
 
     lax.fori_loop(0, batches, batch, 0)
+    slabs, height, chunk = packed_ref.shape
+    for q in range(slabs):
+        packed_ref[q] = rows_ref[pl.ds(q * chunk, chunk), :].T[:height]
 
 
 def spread_kernel(bands, slabs, rows_ref, out_ref, land, send1, recv1, send2, recv2, send3, recv3, send4, recv4, send5, recv5):
     x, b = lax.axis_index("gx"), lax.axis_index("gy")
     partner = b + 1 - 2 * lax.rem(b, 2)
     across = lax.rem(b + 2, bands)
-    chunk = land.shape[1]
-
-    def piece(q):
-        return pl.ds(pl.multiple_of(q * chunk, chunk), chunk)
 
     def slab(k):
         return lax.rem(x + k, slabs)
@@ -96,18 +95,18 @@
 
     def first(k):
         return pltpu.make_async_remote_copy(
-            src_ref=rows_ref.at[piece(slab(k)), :], dst_ref=land.at[k], send_sem=send1.at[k], recv_sem=recv1.at[k],
+            src_ref=rows_ref.at[slab(k)], dst_ref=land.at[k], send_sem=send1.at[k], recv_sem=recv1.at[k],
             device_id={"gx": slab(k)}, device_id_type=MESH,
         )
 
     def second(k):
         return pltpu.make_async_remote_copy(
-            src_ref=out_ref.at[b, piece(x), :], dst_ref=out_ref.at[b, piece(x), :], send_sem=send2.at[k],
+            src_ref=out_ref.at[b, x], dst_ref=out_ref.at[b, x], send_sem=send2.at[k],
             recv_sem=recv2.at[k], device_id={"gx": slab(k)}, device_id_type=MESH,
         )
 
     def hand(k, of_band, send_sem, recv_sem, target):
-        place = out_ref.at[of_band, piece(source(k)), :]
+        place = out_ref.at[of_band, source(k)]
         return pltpu.make_async_remote_copy(
             src_ref=place, dst_ref=place, send_sem=send_sem.at[k], recv_sem=recv_sem.at[k],
             device_id={"gy": target}, device_id_type=MESH,
@@ -136,11 +135,11 @@
     pl.semaphore_wait(barrier, slabs + 1)
 
     each(1, slabs, lambda k: first(k).start())
-    out_ref[b, piece(x), :] = rows_ref[piece(x), :]
+    out_ref[b, x] = rows_ref[x]
 
     def add(k):
         first(k).wait_recv()
-        out_ref[b, piece(x), :] += land[k]
+        out_ref[b, x] += land[k]
 
     each(1, slabs, add)
     fourth(0).start()
@@ -244,9 +243,15 @@
         return pl.ds(pl.multiple_of(t * obs, obs), obs)
 
     cells_s[...] = state_ref[...]
-    for t in range(batches):
-        for q in range(bands):
-            obs_s[pl.ds(t * obs + q * quarter, quarter), :] = obs_ref[q, pl.ds(t * quarter, quarter), :]
+    _, slabs, height, width = obs_ref.shape
+    part = min(width, quarter)
+    for q in range(bands):
+        for p in range(slabs):
+            rest = jnp.zeros((LANES - height, width), F32)
+            block = jnp.concatenate([obs_ref[q, p], rest], axis=0).T
+            for i in range(0, width, part):
+                t, j = divmod(p * width + i, quarter)
+                obs_s[pl.ds(t * obs + q * quarter + j, part), :] = block[i:i + part]
     obs_s[pl.ds(batches * obs, 2 * obs), :] = jnp.zeros((2 * obs, LANES), F32)
     vw_s[...] = jnp.zeros_like(vw_s)
     z3_s[...] = jnp.zeros_like(z3_s)
@@ -329,27 +334,29 @@
     batches, quarter = obs_value.shape
     obs = obs_cell.shape[1]
     slabs, bands = lax.axis_size("gx"), lax.axis_size("gy")
+    chunk = batches * quarter // slabs
+    height = (members + 4 + 7) // 8 * 8
     state, rows = pl.pallas_call(
         functools.partial(pick_kernel, lon_dev, lat_dev),
         out_shape=(
             jax.ShapeDtypeStruct((cells, LANES), F32),
-            jax.ShapeDtypeStruct((batches * quarter, LANES), F32),
+            jax.ShapeDtypeStruct((slabs, height, chunk), F32),
         ),
         in_specs=[SMEM] * 4 + [VMEM] * 2,
         out_specs=(VMEM, VMEM),
+        scratch_shapes=[pltpu.VMEM((batches * quarter, LANES), F32)],
         name="pick",
     )(
         obs_cell, obs_value, owner, order,
         anomalies.reshape(members, classes, levels), state_mean.reshape(classes, levels),
     )
 
-    chunk = batches * quarter // slabs
     rows = pl.pallas_call(
         functools.partial(spread_kernel, bands, slabs),
-        out_shape=jax.ShapeDtypeStruct((bands, batches * quarter, LANES), F32),
+        out_shape=jax.ShapeDtypeStruct((bands, slabs, height, chunk), F32),
         in_specs=[VMEM],
         out_specs=VMEM,
-        scratch_shapes=[pltpu.VMEM((slabs, chunk, LANES), F32)] + [pltpu.SemaphoreType.DMA((slabs,))] * 10,
+        scratch_shapes=[pltpu.VMEM((slabs, height, chunk), F32)] + [pltpu.SemaphoreType.DMA((slabs,))] * 10,
         compiler_params=pltpu.CompilerParams(collective_id=1, has_side_effects=True),
         name="spread",
     )(rows)

time: 134 us -> 127 us (0.948)
  Pallas kernels: 129 us -> 122 us
    pallas_call x1, Pallas kernels: 43 us -> 37.5 us  [local(): pl.pallas_call(functools.partial(spread_kernel, bands, slabs), out_shape=...]
where the time goes in v3:
time: 127 us; the launch traced here: 126 us
  Pallas kernels  122 us (96%)
  local copies, waits for them, and re-layouts  3.26 us (3%)
    pallas_call x1, Pallas kernels, local(): pl.pallas_call(functools.partial(main_kernel, sizes), out_shape=(jax.Shap...  81.3 us
    pallas_call x1, Pallas kernels, local(): pl.pallas_call(functools.partial(spread_kernel, bands, slabs), out_shape=...  37.5 us
    pallas_call x1, Pallas kernels, local(): pl.pallas_call(functools.partial(pick_kernel, lon_dev, lat_dev), out_shap...  3.61 us
    unnamed x2, local copies, waits for them, and re-layouts  3.26 us

profile of v3, /device:TPU:0, one launch (start us, length us, event | category | flops | bytes accessed | tf_op | source)
XLA Modules:
  0.0 126.3 jit_solution(13671221802035948060)
XLA Ops:
  0.6 3.6 %pick.1 = (f32[2048,128]{1,0:T(8,128)}, f32[8,88,128]{2,1,0:T(8,128)}) custom-call(s32[16,256]{1,0:T(8,128)} %cell_ref.1, f32[16,64]{1,0:T(8,128)} %value_ref.1, s32[16]{0:T(128)} %owner_ref.3, s32[16]{0:T(128)} %order_ref.3, f32[80,16,128]{2,1,0:T(8,128)} %bitcast.4, f32[16,128]{1,0:T(8,128)} %bitcast.6), custom_call_target="tpu_custom_call" | custom-call | tf_op jit(solution)/shard_map/pick/pallas_call | solution.py:339
  4.2 37.5 %spread.1.obs_ref = f32[4,8,88,128]{3,2,1,0:T(8,128)} custom-call(f32[8,88,128]{2,1,0:T(8,128)} %get-tuple-element.7.rows_ref), custom_call_target="tpu_custom_call" | custom-call | tf_op jit(solution)/shard_map/spread/pallas_call | solution.py:354
  41.7 81.3 %analysis.1 = (f32[80,16,128]{2,1,0:T(8,128)}, f32[16,128]{1,0:T(8,128)}) custom-call(s32[16]{0:T(128)} %order_ref.3, s32[16]{0:T(128)} %owner_ref.3, f32[2048,128]{1,0:T(8,128)} %get-tuple-element.6.state_ref, f32[4,8,88,128]{3,2,1,0:T(8,128)} %spread.1.obs_ref, s32[16,256]{1,0:T(8,128)} %cell_ref.1, f32[16,64,256]{2,1,0:T(8,128)} %root_ref.1, ...), custom_call_target="tpu_custom_call" | custom-call | tf_op jit(solution)/shard_map/analysis/pallas_call | solution.py:367
  123.0 2.0 %copy.12 = f32[80,2,8,128]{3,2,1,0:T(8,128)} copy(f32[80,2,8,128]{3,2,1,0:T(8,128)} %bitcast.5) | data formatting | bytes 1310720
  125.0 1.3 %copy.13 = f32[2,8,128]{2,1,0:T(8,128)} copy(f32[2,8,128]{2,1,0:T(8,128)} %bitcast.7) | data formatting | bytes 16384
